TPU v7x, 32 devices: a whole 2x2x4 slice. The times are simulated.
32 devices in a mesh: inter: 2 (over y), intra: 16 (over z, x, core).
Axes of the slice: x: 2, y: 2, z: 4, core: 2. Of those that a mesh axis runs over, the one named last changes fastest.
Arguments:
- activations: bfloat16 [65536, 4096], P(('inter', 'intra')), may hold values from -6 to 6
- key_cotangent: bfloat16 [65536, 512], P(('inter', 'intra')), may hold values from -0.046875 to 0.046875
- value_cotangent: bfloat16 [65536, 512], P(('inter', 'intra')), may hold values from -0.046875 to 0.046875
Outputs:
- grad_key: float32 [4096, 512], P('intra')
- grad_value: float32 [4096, 512], P('intra')
All inputs are finite; a program needn't handle non-finite values.
Results may differ from a plain program's by a relative error of at most 0.0029.
Values sent between devices are 32-bit elements; how exact they have to be, the bound alone decides.
A program may use at most 128 MiB of HBM per device.

v0:
```python
import jax
import jax.numpy as jnp
from jax import lax
from jax.sharding import PartitionSpec as P


def term_maker(source, cotangent):
    product = lax.dot_general(
        source, cotangent, (((0,), (0,)), ((), ())), preferred_element_type=jnp.float32
    )
    rounded = lax.optimization_barrier(product.astype(jnp.bfloat16))
    return rounded.astype(jnp.float32)


def local(activations, key_cotangent, value_cotangent):
    cotangent = jnp.concatenate((key_cotangent, value_cotangent), axis=1)
    shard_rows = lax.psum_scatter(
        term_maker(activations, cotangent), "intra", scatter_dimension=0, tiled=True
    )
    shard_rows = lax.psum(shard_rows, "inter")
    half = cotangent.shape[1] // 2
    return (shard_rows[:, :half], shard_rows[:, half:])


def solution(mesh):
    return jax.shard_map(
        local,
        mesh=mesh,
        in_specs=(
            P(("inter", "intra"), None),
            P(("inter", "intra"), None),
            P(("inter", "intra"), None),
        ),
        out_specs=(P("intra", None), P("intra", None)),
        check_vma=False,
    )
```

profile of v0, /device:TPU:0, one launch (start us, length us, event | category | flops | bytes accessed | tf_op | source)
XLA Modules:
  0.0 273.5 jit_solution(9778073993971105029)
XLA Ops:
  7.2 0.0 reduce-scatter.2.cloned.1.call-start
  7.2 23.3 %convert_bitcast_fusion = bf16[4096,1024]{0,1:T(8,128)(2,1)} fusion(bf16[2048,4096]{1,0:T(8,128)(2,1)} %param.3, bf16[2048,512]{1,0:T(8,128)(2,1)} %param.5, bf16[2048,512]{1,0:T(8,128)(2,1)} %param.4), kind=kOutput, calls=%fused_computation | convolution fusion | flops 17192452096 | bytes 29360128 | tf_op jit(solution)/shard_map/dot_general | solution.py:8
  30.5 11.4 %convert_element_type.11 = f32[4096,1024]{0,1:T(8,128)} convert(bf16[4096,1024]{0,1:T(8,128)(2,1)} %convert_bitcast_fusion) | non-fusion elementwise | flops 4194304 | bytes 25165824 | tf_op jit(solution)/shard_map/convert_element_type | solution.py:12
  41.9 0.0 reduce-scatter.2.cloned.1.call-update
  41.9 0.0 all-reduce.2.cloned.1.call-start
  41.9 179.9 %reduce-scatter.2.cloned.1.call-done = f32[256,1024]{0,1:T(8,128)} async-done(((f32[4096,1024]{0,1:T(8,128)}), f32[256,1024]{0,1:T(8,128)}) %reduce-scatter.2.cloned.1.call-update) | async-done | bytes 1048592 | tf_op jit(solution)/shard_map/reduce_scatter | solution.py:17
  221.9 0.0 all-reduce.2.cloned.1.call-update
  221.9 41.5 %all-reduce.2.cloned.1.call-done = f32[256,1024]{0,1:T(8,128)} async-done(((f32[256,1024]{0,1:T(8,128)}), f32[256,1024]{0,1:T(8,128)}) %all-reduce.2.cloned.1.call-update) | async-done | bytes 1048592 | tf_op jit(solution)/shard_map/psum | solution.py:20
  263.4 1.3 fusion.4
  264.7 1.0 copy.6
  265.7 1.0 copy.5
Async XLA Ops:
  7.2 214.7 %reduce-scatter.2.cloned.1.call-start = ((), (), s32[]{:S(2)}) async-start(), calls=%async_computation.1 | async-start | bytes 17825792 | tf_op jit(solution)/shard_map/reduce_scatter | solution.py:17
  41.9 221.5 %all-reduce.2.cloned.1.call-start = ((), (), s32[]{:S(2)}) async-start(), calls=%async_computation.2 | async-start | bytes 2097152 | tf_op jit(solution)/shard_map/psum | solution.py:20
Sparse Core Ops, SparseCore 0:
  42.0 179.8 reduce-scatter.1
  224.2 39.1 all-reduce.1
where the time goes:
time: 274 us
  waiting for transfers between devices  221 us (81%)
  matrix products  23.3 us (9%)
  between operations  14 us (5%)
  other arithmetic  11.4 us (4%)
  local copies, waits for them, and re-layouts  3.26 us (1%)
    reduce_scatter x1, waiting for transfers between devices, local(): lax.psum_scatter(term_maker(activations, cotangent), 'intra', scatter_dim...  180 us
    psum x1, waiting for transfers between devices, local(): shard_rows = lax.psum(shard_rows, 'inter')  41.5 us
    dot_general x1, matrix products, term_maker(): lax.dot_general(source, cotangent, (((0,), (0,)), ((), ())), preferred_el...  23.3 us
    convert_element_type x1, other arithmetic, term_maker(): return rounded.astype(jnp.float32)  11.4 us
  transfers between devices with their start and end apart: 2, of which 2 were waited for; matrix products, arithmetic and copies ran while one was open for 0% of the time, Pallas kernels for 0%

commit v1 on v0

v1 whole, which is shorter than its diff:
```python
import functools
import heapq

import jax
import jax.numpy as jnp
from jax import lax
from jax.experimental import pallas as pl
from jax.experimental.pallas import tpu as pltpu
from jax.sharding import PartitionSpec as P

MESH = pl.DeviceIdType.MESH


class Message:
    def __init__(self, part, stage, axis, block, target, width, split):
        self.part, self.stage, self.axis = part, stage, axis
        self.block, self.target, self.width, self.split = block, target, width, split
        self.slot = None


def plan_messages(groups, columns):
    bits = tuple(("z", b) for b in range(groups.bit_length() - 1))
    x, y, gather, both = ("x", 0), ("y", 0), ("gather", 0), ("both", 0)
    parts = (
        (0, columns // 2, (x, y) + bits + (gather,)),
        (columns // 2, columns // 4, (y, x) + bits + (gather,)),
        (3 * columns // 4, columns // 4, bits + (x, both)),
    )
    messages = []
    for part, (_, width, stages) in enumerate(parts):
        live, split = list(range(2 * groups)), False
        for stage, axis in enumerate(stages):
            kind, bit = axis
            if kind == "y":
                width, split = width // 2, True
                messages += [Message(part, stage, axis, k, k, width, split) for k in live]
            elif kind in ("gather", "both"):
                messages.append(Message(part, stage, axis, 0, 0, width, split))
            else:
                step = 1 if kind == "x" else 2 << bit
                sent = [k for k in live if k & step]
                messages += [Message(part, stage, axis, k, k - step, width, split) for k in sent]
                live = [k for k in live if not k & step]
    counts = {}
    for message in messages:
        message.slot = counts.get(message.width, 0)
        counts[message.width] = message.slot + 1
    return parts, messages, counts


def block_order(groups):
    return sorted(range(2 * groups), key=lambda k: (-((k >> 1) & 1) - (k & 1), -((k >> 1) & 1), -k))


def schedule(messages, order, rows):
    sends = {(m.part, m.block): [] for m in messages}
    for m in messages:
        sends[m.part, m.block].append(m)
    ready_at = {k: 4.0 + 2.7 * (i + 1) for i, k in enumerate(order)}
    link_free, heap, handled, done = {}, [], [], set()

    def needed(message):
        return [
            o
            for o in messages
            if o.part == message.part and o.target == message.block and o.stage < message.stage
        ]

    def issue(message, now):
        link = "y" if message.axis[0] in ("y", "gather", "both") else message.axis[0]
        start = max(now, link_free.get(link, 0.0))
        link_free[link] = start + message.width * rows * 4 / 46.6e3
        heapq.heappush(heap, (link_free[link] + 2.0, messages.index(message), message))

    initial = {k: [m for m in messages if m.block == k and not needed(m)] for k in order}
    waiting = [m for m in messages if needed(m)]
    for k in order:
        for m in initial[k]:
            issue(m, ready_at[k])
    loop_end = max(ready_at.values()) + 2.0
    now = loop_end
    actions = []
    while heap:
        at, _, message = heapq.heappop(heap)
        now = max(now, at)
        done.add(message)
        follow = [m for m in waiting if all(o in done for o in needed(m))]
        waiting = [m for m in waiting if m not in follow]
        for m in follow:
            issue(m, now)
        actions.append((message, follow))
    return initial, actions


def kernel(
    mesh_shape, plan, order, steps,
    a_hbm, key_hbm, value_hbm, key_out, value_out,
    a_ref, cot_ref, pair_ref, mate_ref, wide_ref, half_ref, quarter_ref,
    a_sem, cot_sem, mate_send, mate_recv, send_sem, recv_sem,
):
    parts, messages = plan
    initial, actions = steps
    groups = mesh_shape["intra"] // 4
    blocks = 2 * groups
    rows = key_out.shape[0]
    tall = 2 * rows
    half = key_hbm.shape[1]
    landing = {ref.shape[2]: ref for ref in (wide_ref, half_ref, quarter_ref)}

    y = lax.axis_index("inter")
    me = lax.axis_index("intra")
    core = me % 2
    x = (me // 2) % 2
    group = me // 4

    def flipped(k):
        place = (x + k % 2) % 2
        for b in range(groups.bit_length() - 1):
            place = place + 2 * (1 << b) * ((group // (1 << b) + k // (2 << b)) % 2)
        return place

    def partner(axis):
        kind, bit = axis
        if kind == "core":
            return {"intra": me + 1 - 2 * core}
        if kind == "x":
            return {"intra": me + 2 * (1 - 2 * x)}
        if kind == "z":
            return {"intra": me + (4 << bit) * (1 - 2 * ((group // (1 << bit)) % 2))}
        return {"inter": 1 - y}

    cot_copies = [
        pltpu.make_async_copy(key_hbm, cot_ref.at[:, pl.ds(0, half)], cot_sem.at[0]),
        pltpu.make_async_copy(value_hbm, cot_ref.at[:, pl.ds(half, half)], cot_sem.at[1]),
    ]
    for copy in cot_copies:
        copy.start()

    def a_copy(i, k):
        columns = pl.ds(pl.multiple_of(flipped(k) * tall, tall), tall)
        return pltpu.make_async_copy(a_hbm.at[:, columns], a_ref.at[i], a_sem.at[i])

    for i, k in enumerate(order):
        a_copy(i, k).start()

    barrier = pltpu.get_barrier_semaphore()
    neighbours = [("core", 0), ("x", 0), ("y", 0)]
    neighbours += [("z", b) for b in range(groups.bit_length() - 1)]
    for axis in neighbours:
        pl.semaphore_signal(barrier, inc=1, device_id=partner(axis), device_id_type=MESH)
    pl.semaphore_wait(barrier, len(neighbours))

    def mate_copy(i):
        return pltpu.make_async_remote_copy(
            src_ref=pair_ref.at[i, 1 - core],
            dst_ref=mate_ref.at[i],
            send_sem=mate_send.at[i],
            recv_sem=mate_recv.at[i],
            device_id=partner(("core", 0)),
            device_id_type=MESH,
        )

    place = {k: i for i, k in enumerate(order)}

    def columns_of(message, mine):
        base, width, _ = parts[message.part]
        if not message.split:
            return pl.ds(base, width)
        side = y if mine else 1 - y
        return pl.ds(pl.multiple_of(base + side * message.width, 128), message.width)

    def remote(message):
        number = messages.index(message)
        mine = message.axis[0] != "y"
        return pltpu.make_async_remote_copy(
            src_ref=pair_ref.at[place[message.block], core, :, columns_of(message, mine)],
            dst_ref=landing[message.width].at[message.slot],
            send_sem=send_sem.at[number],
            recv_sem=recv_sem.at[number],
            device_id=partner(message.axis),
            device_id_type=MESH,
        )

    def finish(i):
        mate_copy(i).wait_recv()
        pair_ref[i, core] += mate_ref[i]
        for j, k in enumerate(order):
            @pl.when(i == j)
            def _():
                for message in initial[k]:
                    remote(message).start()

    for copy in cot_copies:
        copy.wait()

    def body(i, carry):
        pltpu.make_async_copy(
            a_hbm.at[:, pl.ds(0, tall)], a_ref.at[i], a_sem.at[i]
        ).wait()
        product = lax.dot_general(
            a_ref[i], cot_ref[...], (((0,), (0,)), ((), ())),
            preferred_element_type=jnp.float32,
        )
        rounded = product.astype(jnp.bfloat16).astype(jnp.float32)
        pair_ref[i] = rounded.reshape(2, rows, 2 * half)
        mate_copy(i).start()

        @pl.when(i > 0)
        def _():
            finish(i - 1)

        return carry

    lax.fori_loop(0, blocks, body, 0)
    finish(blocks - 1)

    def result(base, width):
        if base < half:
            return key_out, pl.ds(base, width)
        return value_out, pl.ds(base - half, width)

    first = place[0]
    for message, follow in actions:
        remote(message).wait_recv()
        base, width, _ = parts[message.part]
        arrived = landing[message.width].at[message.slot]
        kind = message.axis[0]
        if kind == "both":
            out, columns = result(base, width)
            out[:, columns] = pair_ref[first, core, :, pl.ds(base, width)] + arrived[...]
        elif kind == "gather":
            out = result(base, width)[0]
            start = base if base < half else base - half
            columns = pl.ds(pl.multiple_of(start + (1 - y) * message.width, 128), message.width)
            out[:, columns] = arrived[...]
        else:
            i = place[message.target]
            columns = columns_of(message, True)
            pair_ref[i, core, :, columns] += arrived[...]
        for later in follow:
            remote(later).start()
            if later.axis[0] == "gather":
                base, width, _ = parts[later.part]
                out = result(base, width)[0]
                start = base if base < half else base - half
                columns = pl.ds(pl.multiple_of(start + y * later.width, 128), later.width)
                out[:, columns] = pair_ref[first, core, :, columns_of(later, True)]

    for i in range(blocks):
        mate_copy(i).wait_send()
    for message in messages:
        remote(message).wait_send()


def local(mesh_shape, activations, key_cotangent, value_cotangent):
    tokens, width = activations.shape
    half = key_cotangent.shape[1]
    rows = width // mesh_shape["intra"]
    groups = mesh_shape["intra"] // 4
    blocks = 2 * groups
    parts, messages, counts = plan_messages(groups, 2 * half)
    order = block_order(groups)
    steps = schedule(messages, order, rows)
    f32 = jnp.float32
    landing = [pltpu.VMEM((counts[w], rows, w), f32) for w in sorted(counts, reverse=True)]
    shape = jax.ShapeDtypeStruct((rows, half), f32)
    return pl.pallas_call(
        functools.partial(kernel, mesh_shape, (parts, messages), order, steps),
        out_shape=(shape, shape),
        in_specs=[pl.BlockSpec(memory_space=pl.ANY)] * 3,
        out_specs=(pl.BlockSpec(memory_space=pltpu.VMEM),) * 2,
        scratch_shapes=[
            pltpu.VMEM((blocks, tokens, 2 * rows), activations.dtype),
            pltpu.VMEM((tokens, 2 * half), key_cotangent.dtype),
            pltpu.VMEM((blocks, 2, rows, 2 * half), f32),
            pltpu.VMEM((blocks, rows, 2 * half), f32),
            *landing,
            pltpu.SemaphoreType.DMA((blocks,)),
            pltpu.SemaphoreType.DMA((2,)),
            pltpu.SemaphoreType.DMA((blocks,)),
            pltpu.SemaphoreType.DMA((blocks,)),
            pltpu.SemaphoreType.DMA((len(messages),)),
            pltpu.SemaphoreType.DMA((len(messages),)),
        ],
        compiler_params=pltpu.CompilerParams(
            collective_id=0, has_side_effects=True, vmem_limit_bytes=67043328
        ),
    )(activations, key_cotangent, value_cotangent)


def solution(mesh):
    mesh_shape = dict(mesh.shape)
    return jax.shard_map(
        functools.partial(local, mesh_shape),
        mesh=mesh,
        in_specs=(
            P(("inter", "intra"), None),
            P(("inter", "intra"), None),
            P(("inter", "intra"), None),
        ),
        out_specs=(P("intra", None), P("intra", None)),
        check_vma=False,
    )
```

time: 274 us -> 95.1 us (0.35)
  waiting for transfers between devices: 221 us -> 0 us
  Pallas kernels: 0 us -> 90.6 us
  matrix products: 23.3 us -> 0 us
  between operations: 14 us -> 0.64 us
  other arithmetic: 11.4 us -> 0 us
    reduce_scatter x1 -> x0, waiting for transfers between devices: 180 us -> none  [local(): lax.psum_scatter(term_maker(activations, cotangent), 'intra', scatter_dim...]
    pallas_call x0 -> x1, Pallas kernels: none -> 90.6 us  [local(): pl.pallas_call(functools.partial(kernel, mesh_shape, (parts, messages), o...]
    psum x1 -> x0, waiting for transfers between devices: 41.5 us -> none  [local(): shard_rows = lax.psum(shard_rows, 'inter')]
    dot_general x1 -> x0, matrix products: 23.3 us -> none  [term_maker(): lax.dot_general(source, cotangent, (((0,), (0,)), ((), ())), preferred_el...]
    convert_element_type x1 -> x0, other arithmetic: 11.4 us -> none  [term_maker(): return rounded.astype(jnp.float32)]
  transfers between devices with their start and end apart: 2 -> 0, of which waited for: 2 -> 0; matrix products, arithmetic and copies ran while one was open for 0% -> 0% of each run, Pallas kernels for 0% -> 0%
where the time goes in v1:
time: 95.1 us; the launch traced here: 94.9 us
  Pallas kernels  90.6 us (95%)
  local copies, waits for them, and re-layouts  3.74 us (4%)
    pallas_call x1, Pallas kernels, local(): pl.pallas_call(functools.partial(kernel, mesh_shape, (parts, messages), o...  90.6 us
    unnamed x2, local copies, waits for them, and re-layouts  3.74 us

profile of v1, /device:TPU:0, one launch (start us, length us, event | category | flops | bytes accessed | tf_op | source)
XLA Modules:
  0.0 94.9 jit_solution(3099887396316343084)
XLA Ops:
  0.6 90.6 %shard_map.50 = (f32[256,512]{1,0:T(8,128)}, f32[256,512]{1,0:T(8,128)}) custom-call(bf16[2048,4096]{1,0:T(8,128)(2,1)} %a_hbm.1, bf16[2048,512]{1,0:T(8,128)(2,1)} %key_hbm.1, bf16[2048,512]{1,0:T(8,128)(2,1)} %value_hbm.1), custom_call_target="tpu_custom_call" | custom-call | tf_op jit(solution)/shard_map/pallas_call | solution.py:267
  91.2 1.9 %copy.7 = f32[256,512]{1,0:T(8,128)} copy(f32[256,512]{1,0:T(8,128)} %get-tuple-element.4) | data formatting | bytes 1048576
  93.1 1.9 %copy.8 = f32[256,512]{1,0:T(8,128)} copy(f32[256,512]{1,0:T(8,128)} %get-tuple-element.5) | data formatting | bytes 1048576

commit v2 on v1

--- a/solution.py
+++ b/solution.py
@@ -53,11 +53,10 @@
 
 
 def schedule(messages, order, rows):
-    sends = {(m.part, m.block): [] for m in messages}
-    for m in messages:
-        sends[m.part, m.block].append(m)
-    ready_at = {k: 4.0 + 2.7 * (i + 1) for i, k in enumerate(order)}
-    link_free, heap, handled, done = {}, [], [], set()
+    ready_at = {
+        (k, h): 4.5 + 1.7 * (2 * i + h + 1) for i, k in enumerate(order) for h in range(2)
+    }
+    latency, depth = 2.0, {"x": 3, "z": len(order)}
 
     def needed(message):
         return [
@@ -66,29 +65,59 @@
             if o.part == message.part and o.target == message.block and o.stage < message.stage
         ]
 
-    def issue(message, now):
-        link = "y" if message.axis[0] in ("y", "gather", "both") else message.axis[0]
-        start = max(now, link_free.get(link, 0.0))
-        link_free[link] = start + message.width * rows * 4 / 46.6e3
-        heapq.heappush(heap, (link_free[link] + 2.0, messages.index(message), message))
-
-    initial = {k: [m for m in messages if m.block == k and not needed(m)] for k in order}
+    def length(message):
+        far = 2 if message.axis[0] == "z" and message.axis[1] else 1
+        return far * message.width * rows * 4 / 46.6e3
+
+    @functools.cache
+    def tail(message):
+        after = [
+            latency + length(o) + tail(o)
+            for o in messages
+            if o.part == message.part and o.block == message.target and o.stage > message.stage
+        ]
+        return max(after, default=0.0)
+
+    def link(message):
+        return "y" if message.axis[0] in ("y", "gather", "both") else message.axis[0]
+
+    initial, actions, done, heap = {}, [], set(), []
+    link_free, flying, queued = {}, {}, {"x": [], "z": []}
+
+    def issue(ready, now):
+        started = []
+        for message in ready:
+            if link(message) in queued:
+                queued[link(message)].append(message)
+            else:
+                started.append(message)
+        for name, queue in queued.items():
+            queue.sort(key=tail, reverse=True)
+            while queue and flying.get(name, 0) < depth[name]:
+                started.append(queue.pop(0))
+                flying[name] = flying.get(name, 0) + 1
+        for message in started:
+            begin = max(now, link_free.get(link(message), 0.0))
+            link_free[link(message)] = begin + length(message)
+            arrival = begin + length(message) + latency
+            heapq.heappush(heap, (arrival, messages.index(message), message))
+        return started
+
+    for k, h in ready_at:
+        mine = [m for m in messages if m.block == k and (m.part > 0) == h and not needed(m)]
+        initial[k, h] = issue(mine, ready_at[k, h])
     waiting = [m for m in messages if needed(m)]
-    for k in order:
-        for m in initial[k]:
-            issue(m, ready_at[k])
-    loop_end = max(ready_at.values()) + 2.0
-    now = loop_end
-    actions = []
+    now = max(ready_at.values())
+    depth["z"] = 2
     while heap:
         at, _, message = heapq.heappop(heap)
         now = max(now, at)
         done.add(message)
-        follow = [m for m in waiting if all(o in done for o in needed(m))]
-        waiting = [m for m in waiting if m not in follow]
-        for m in follow:
-            issue(m, now)
-        actions.append((message, follow))
+        if link(message) in queued:
+            flying[link(message)] -= 1
+        ready = [m for m in waiting if all(o in done for o in needed(m))]
+        waiting = [m for m in waiting if m not in ready]
+        actions.append((message, issue(ready, now)))
     return initial, actions
 
 
@@ -133,15 +162,13 @@
         pltpu.make_async_copy(key_hbm, cot_ref.at[:, pl.ds(0, half)], cot_sem.at[0]),
         pltpu.make_async_copy(value_hbm, cot_ref.at[:, pl.ds(half, half)], cot_sem.at[1]),
     ]
-    for copy in cot_copies:
-        copy.start()
+    cot_copies[0].start()
 
     def a_copy(i, k):
         columns = pl.ds(pl.multiple_of(flipped(k) * tall, tall), tall)
         return pltpu.make_async_copy(a_hbm.at[:, columns], a_ref.at[i], a_sem.at[i])
 
-    for i, k in enumerate(order):
-        a_copy(i, k).start()
+    a_copy(0, order[0]).start()
 
     barrier = pltpu.get_barrier_semaphore()
     neighbours = [("core", 0), ("x", 0), ("y", 0)]
@@ -150,12 +177,15 @@
         pl.semaphore_signal(barrier, inc=1, device_id=partner(axis), device_id_type=MESH)
     pl.semaphore_wait(barrier, len(neighbours))
 
-    def mate_copy(i):
+    def side(h):
+        return pl.ds(h * half, half)
+
+    def mate_copy(i, h):
         return pltpu.make_async_remote_copy(
-            src_ref=pair_ref.at[i, 1 - core],
-            dst_ref=mate_ref.at[i],
-            send_sem=mate_send.at[i],
-            recv_sem=mate_recv.at[i],
+            src_ref=pair_ref.at[i, 1 - core, :, side(h)],
+            dst_ref=mate_ref.at[i, h],
+            send_sem=mate_send.at[i, h],
+            recv_sem=mate_recv.at[i, h],
             device_id=partner(("core", 0)),
             device_id_type=MESH,
         )
@@ -181,38 +211,57 @@
             device_id_type=MESH,
         )
 
-    def finish(i):
-        mate_copy(i).wait_recv()
-        pair_ref[i, core] += mate_ref[i]
+    def finish(i, h):
+        mate_copy(i, h).wait_recv()
+        pair_ref[i, core, :, side(h)] += mate_ref[i, h]
         for j, k in enumerate(order):
-            @pl.when(i == j)
-            def _():
-                for message in initial[k]:
-                    remote(message).start()
-
-    for copy in cot_copies:
-        copy.wait()
+            if initial[k, h]:
+                @pl.when(i == j)
+                def _():
+                    for message in initial[k, h]:
+                        remote(message).start()
+
+    def multiply(i, h):
+        product = lax.dot_general(
+            a_ref[i], cot_ref[:, side(h)], (((0,), (0,)), ((), ())),
+            preferred_element_type=jnp.float32,
+        )
+        rounded = product.astype(jnp.bfloat16).astype(jnp.float32)
+        pair_ref[i, :, :, side(h)] = rounded.reshape(2, rows, half)
+        mate_copy(i, h).start()
+
+    cot_copies[0].wait()
 
     def body(i, carry):
         pltpu.make_async_copy(
             a_hbm.at[:, pl.ds(0, tall)], a_ref.at[i], a_sem.at[i]
         ).wait()
-        product = lax.dot_general(
-            a_ref[i], cot_ref[...], (((0,), (0,)), ((), ())),
-            preferred_element_type=jnp.float32,
-        )
-        rounded = product.astype(jnp.bfloat16).astype(jnp.float32)
-        pair_ref[i] = rounded.reshape(2, rows, 2 * half)
-        mate_copy(i).start()
+
+        @pl.when(i == 0)
+        def _():
+            cot_copies[1].start()
+
+        for j, k in enumerate(order[1:]):
+            @pl.when(i == j)
+            def _():
+                a_copy(j + 1, k).start()
+
+        multiply(i, 0)
 
         @pl.when(i > 0)
         def _():
-            finish(i - 1)
-
+            finish(i - 1, 1)
+
+        @pl.when(i == 0)
+        def _():
+            cot_copies[1].wait()
+
+        multiply(i, 1)
+        finish(i, 0)
         return carry
 
     lax.fori_loop(0, blocks, body, 0)
-    finish(blocks - 1)
+    finish(blocks - 1, 1)
 
     def result(base, width):
         if base < half:
@@ -247,7 +296,8 @@
                 out[:, columns] = pair_ref[first, core, :, columns_of(later, True)]
 
     for i in range(blocks):
-        mate_copy(i).wait_send()
+        for h in range(2):
+            mate_copy(i, h).wait_send()
     for message in messages:
         remote(message).wait_send()
 
@@ -273,12 +323,12 @@
             pltpu.VMEM((blocks, tokens, 2 * rows), activations.dtype),
             pltpu.VMEM((tokens, 2 * half), key_cotangent.dtype),
             pltpu.VMEM((blocks, 2, rows, 2 * half), f32),
-            pltpu.VMEM((blocks, rows, 2 * half), f32),
+            pltpu.VMEM((blocks, 2, rows, half), f32),
             *landing,
             pltpu.SemaphoreType.DMA((blocks,)),
             pltpu.SemaphoreType.DMA((2,)),
-            pltpu.SemaphoreType.DMA((blocks,)),
-            pltpu.SemaphoreType.DMA((blocks,)),
+            pltpu.SemaphoreType.DMA((blocks, 2)),
+            pltpu.SemaphoreType.DMA((blocks, 2)),
             pltpu.SemaphoreType.DMA((len(messages),)),
             pltpu.SemaphoreType.DMA((len(messages),)),
         ],

time: 95.1 us -> 94.3 us (level)
  no operation moved by 1% of the time
where the time goes in v2:
time: 94.3 us; the launch traced here: 94 us
  Pallas kernels  89.7 us (95%)
  local copies, waits for them, and re-layouts  3.74 us (4%)
    pallas_call x1, Pallas kernels, local(): pl.pallas_call(functools.partial(kernel, mesh_shape, (parts, messages), o...  89.7 us
    unnamed x2, local copies, waits for them, and re-layouts  3.74 us

profile of v2, /device:TPU:0, one launch (start us, length us, event | category | flops | bytes accessed | tf_op | source)
XLA Modules:
  0.0 94.0 jit_solution(4186863523457555952)
XLA Ops:
  0.6 89.7 %shard_map.50 = (f32[256,512]{1,0:T(8,128)}, f32[256,512]{1,0:T(8,128)}) custom-call(bf16[2048,4096]{1,0:T(8,128)(2,1)} %a_hbm.1, bf16[2048,512]{1,0:T(8,128)(2,1)} %key_hbm.1, bf16[2048,512]{1,0:T(8,128)(2,1)} %value_hbm.1), custom_call_target="tpu_custom_call" | custom-call | tf_op jit(solution)/shard_map/pallas_call | solution.py:317
  90.3 1.9 %copy.7 = f32[256,512]{1,0:T(8,128)} copy(f32[256,512]{1,0:T(8,128)} %get-tuple-element.4) | data formatting | bytes 1048576
  92.2 1.9 %copy.8 = f32[256,512]{1,0:T(8,128)} copy(f32[256,512]{1,0:T(8,128)} %get-tuple-element.5) | data formatting | bytes 1048576
